TPU v7x, 32 devices: a whole 2x2x4 slice. The times are simulated.
32 devices in a mesh: row: 8 (over z, y), col: 4 (over x, core).
Axes of the slice: x: 2, y: 2, z: 4, core: 2. Of those that a mesh axis runs over, the one named last changes fastest.
Arguments:
- features: bfloat16 [6144, 4096], P(('row', 'col')), may hold values from -6 to 6
- cotangent: bfloat16 [6144, 8192], P(('row', 'col')), may hold values from -0.078125 to 0.078125
Outputs:
- weight_grad: float32 [4096, 8192], P('row', 'col')
All inputs are finite; a program needn't handle non-finite values.
Results may differ from a plain program's by a relative error of at most 0.0003.
Values may be sent and summed in bfloat16 or wider, within the bound.
A program may use at most 256 MiB of HBM per device.

v0:
```python
import functools

import jax
import jax.numpy as jnp
from jax import lax
from jax.experimental import pallas as pl
from jax.experimental.pallas import tpu as pltpu
from jax.sharding import PartitionSpec as P

MESH = pl.DeviceIdType.MESH
CHUNK = 512
AHEAD = 2
LAG = 1
E_LAG = 1
VMEM_MOST = 60 * 1024 * 1024


def tokens_product(left, right):
    return lax.dot_general(
        left, right, (((0,), (0,)), ((), ())), preferred_element_type=jnp.float32
    )


def plain(features, cotangent):
    row_count = lax.axis_size("row")
    width_in = features.shape[1]
    local_rows = width_in // row_count
    columns = lax.all_to_all(cotangent, "col", split_axis=1, concat_axis=0, tiled=True)
    tok_local = features.shape[0]
    exchanged = lax.all_to_all(features, "row", split_axis=1, concat_axis=0, tiled=True)
    stacked = exchanged.reshape(row_count, tok_local, local_rows)
    gathered = lax.all_gather(stacked, "col", axis=1, tiled=True)
    all_tokens = gathered.reshape(-1, local_rows)
    return tokens_product(all_tokens, lax.all_gather(columns, "row", axis=0, tiled=True))


def partial_chunks(chunks):
    return tuple(j for j in range(2, chunks - 1) if j % 3 != 1)


def kernel(
    lines, cols, part, feat, cot, out,
    fall, fend, dall, ysend, yrecv, acc, esend, erecv, eacc, eland,
    f_loc, d_loc, fz_s, fz_r, f2_r, fr_s, gx_s, gx_r, gm_s, gm_r, dx_s, dx_r,
    rz_s, lz_s, z_r, y_s, y_r, ey_s, ey_r, ez_s, ez_r, o_s,
):
    row = lax.axis_index("row")
    col = lax.axis_index("col")
    z, y = row // 2, row % 2
    tok = feat.shape[0]
    rows = fall.shape[1]
    half = rows // 2
    chunks = dall.shape[0]
    width = chunks * CHUNK
    plane = tok * cols
    chips = cols // 2
    mate = col + 1 - 2 * (col % 2)
    last = lines - 1
    is_end = (z == 0) | (z == last)
    helps = (z == 1) | (z == last - 1)
    end = jnp.where(z * 2 < lines, 0, last)

    def at_z(other):
        return {"row": other * 2 + y, "col": col}

    def at_col(other):
        return {"row": row, "col": other}

    partner = {"row": z * 2 + (1 - y), "col": col}

    def remote(src, dst, s, r, dev):
        return pltpu.make_async_remote_copy(
            src_ref=src, dst_ref=dst, send_sem=s, recv_sem=r,
            device_id=dev, device_id_type=MESH,
        )

    barrier = pltpu.get_barrier_semaphore()
    for d in range(1, lines):
        pl.semaphore_signal(barrier, inc=1, device_id=at_z((z + d) % lines), device_id_type=MESH)
    for d in range(1, cols):
        pl.semaphore_signal(barrier, inc=1, device_id=at_col((col + d) % cols), device_id_type=MESH)
    pl.semaphore_signal(barrier, inc=1, device_id=partner, device_id_type=MESH)
    pl.semaphore_wait(barrier, lines + cols - 1)

    def mine(zz, cc):
        return pl.ds(pl.multiple_of((zz * cols + cc) * tok, tok), tok)

    def f_cols(zz):
        return feat.at[:, pl.ds(pl.multiple_of(zz * rows, rows), rows)]

    def f_send(zz):
        return remote(f_cols(zz), fall.at[mine(z, col)], fz_s.at[zz], fz_r.at[z], at_z(zz))

    def f_send_end(zz):
        to = jnp.where(zz == 0, 1, last - 1)
        return remote(f_cols(zz), fend.at[mine(z, col)], fz_s.at[zz], f2_r.at[z], at_z(to))

    def f_recv(zz):
        return remote(f_cols(z), fall.at[mine(zz, col)], fz_s.at[zz], fz_r.at[zz], at_z(zz))

    def f_recv_end(zz):
        return remote(f_cols(z), fend.at[mine(zz, col)], fz_s.at[zz], f2_r.at[zz], at_z(zz))

    def f_relay(zz):
        return remote(
            fend.at[mine(zz, col)], fall.at[mine(zz, col)], fr_s.at[zz], fz_r.at[zz], at_z(end)
        )

    held = (fall, fend)

    def g_send(b, zz, k):
        block = held[b].at[mine(zz, col)]
        return remote(
            block, block, gx_s.at[b, zz, k], gx_r.at[b, zz, k], at_col((col + 2 * k) % cols)
        )

    def g_recv(b, zz, k):
        block = held[b].at[mine(zz, (col + cols - 2 * k) % cols)]
        return remote(
            block, block, gx_s.at[b, zz, k], gx_r.at[b, zz, k], at_col((col + 2 * k) % cols)
        )

    def m_send(b, zz, k):
        block = held[b].at[mine(zz, (col + cols - 2 * k) % cols)]
        return remote(block, block, gm_s.at[b, zz, k], gm_r.at[b, zz, k], at_col(mate))

    def m_recv(b, zz, k):
        block = held[b].at[mine(zz, (mate + cols - 2 * k) % cols)]
        return remote(block, block, gm_s.at[b, zz, k], gm_r.at[b, zz, k], at_col(mate))

    def gather_start(b, zz):
        for k in range(1, chips):
            g_send(b, zz, k).start()
        m_send(b, zz, 0).start()

    def gather_forward(b, zz):
        for k in range(1, chips):
            g_recv(b, zz, k).wait_recv()
            m_send(b, zz, k).start()

    def gather_end(b, zz):
        for k in range(chips):
            m_recv(b, zz, k).wait_recv()

    def gather_drain(b, zz):
        for k in range(1, chips):
            g_send(b, zz, k).wait_send()
        for k in range(chips):
            m_send(b, zz, k).wait_send()

    def d_cols(cc, j):
        return cot.at[:, pl.ds(pl.multiple_of(cc * width + j * CHUNK, CHUNK), CHUNK)]

    def d_send(j, d):
        to = (col + d) % cols
        return remote(
            d_cols(to, j), dall.at[j, mine(z, col)], dx_s.at[j, d], dx_r.at[j, d], at_col(to)
        )

    def d_recv(j, d):
        block = dall.at[j, mine(z, (col + cols - d) % cols)]
        return remote(block, block, dx_s.at[j, d], dx_r.at[j, d], at_col((col + d) % cols))

    def plane_of(j, zz):
        return dall.at[j, pl.ds(pl.multiple_of(zz * plane, plane), plane)]

    def z_right(j, zz):
        return remote(plane_of(j, zz), plane_of(j, zz), rz_s.at[j, zz], z_r.at[j, zz], at_z((z + 1) % lines))

    def z_left(j, zz):
        return remote(plane_of(j, zz), plane_of(j, zz), lz_s.at[j, zz], z_r.at[j, zz], at_z((z + last) % lines))

    def most(j):
        return last - 1 if j in part else last

    def least(j):
        return 1 if j in part else 0

    f_own = pltpu.make_async_copy(f_cols(z), fall.at[mine(z, col)], f_loc.at[0])
    f_own.start()
    f_own_end = pltpu.make_async_copy(f_cols(end), fend.at[mine(z, col)], f_loc.at[1])

    @pl.when(helps)
    def _():
        f_own_end.start()

    for j in range(chunks):
        pltpu.make_async_copy(d_cols(col, j), dall.at[j, mine(z, col)], d_loc.at[j]).start()

    def by_helper(zz):
        return ((zz == 0) & (z != 1)) | ((zz == last) & (z != last - 1))

    for via in (False, True):
        for d in range(last, 0, -1):
            for zz in (z + d, z - d):
                inside = (zz >= 0) & (zz < lines)

                @pl.when(inside & by_helper(zz) if via else inside & ~by_helper(zz))
                def _():
                    (f_send_end if via else f_send)(zz).start()

    ahead = min(AHEAD, chunks)
    for j in range(ahead):
        for d in range(1, cols):
            d_send(j, d).start()
    f_own.wait()
    gather_start(0, z)

    def send_own(j):
        pltpu.make_async_copy(d_cols(col, j), dall.at[j, mine(z, col)], d_loc.at[j]).wait()
        for d in range(1, cols):
            d_recv(j, d).wait_recv()

        @pl.when(z < most(j))
        def _():
            z_right(j, z).start()

        @pl.when(z > least(j))
        def _():
            z_left(j, z).start()

    def relay(j):
        for d in range(1, lines):
            @pl.when((z - d >= 0) & (z <= most(j)))
            def _():
                z_right(j, z - d).wait_recv()

                @pl.when(z < most(j))
                def _():
                    z_right(j, z - d).start()

            @pl.when((z + d < lines) & (z >= least(j)))
            def _():
                z_left(j, z + d).wait_recv()

                @pl.when(z > least(j))
                def _():
                    z_left(j, z + d).start()

    tile = min(CHUNK, half)

    def product(left, j, into, at, which, start, length):
        span = pl.ds(pl.multiple_of(start, plane), length)

        @pl.loop(0, half // tile)
        def _(m):
            begin = pl.multiple_of(which * half + m * tile, tile)
            into[at, pl.ds(pl.multiple_of(m * tile, tile), tile), :] = tokens_product(
                left[span, pl.ds(begin, tile)], dall[j, span]
            )

    def y_copy(j):
        return remote(ysend.at[j], yrecv.at[j], y_s.at[j], y_r.at[j], partner)

    def out_copy(j):
        return pltpu.make_async_copy(acc.at[j], out.at[:, pl.ds(j * CHUNK, CHUNK)], o_s.at[j])

    def multiply(j):
        if j in part:
            @pl.when(is_end)
            def _():
                product(fall, j, ysend, j, 1 - y, z * plane, plane)
                product(fall, j, acc, j, y, z * plane, plane)

            @pl.when(~is_end)
            def _():
                product(fall, j, ysend, j, 1 - y, 0, lines * plane)
                product(fall, j, acc, j, y, 0, lines * plane)
        else:
            product(fall, j, ysend, j, 1 - y, 0, lines * plane)
            product(fall, j, acc, j, y, 0, lines * plane)
        y_copy(j).start()

    def finish(j):
        y_copy(j).wait()
        acc[j] += yrecv[j]
        if j in part:
            @pl.when(~is_end)
            def _():
                out_copy(j).start()
        else:
            out_copy(j).start()

    def e_copy(p):
        return remote(esend.at[p], erecv.at[p], ey_s.at[p], ey_r.at[p], partner)

    def e_move(p):
        return remote(eacc.at[p], eland.at[p], ez_s.at[p], ez_r.at[p], at_z(end))

    def extra(p):
        @pl.when(helps)
        def _():
            start = jnp.where(end == 0, plane, 0)
            product(fend, part[p], esend, p, 1 - y, start, last * plane)
            product(fend, part[p], eacc, p, y, start, last * plane)
            e_copy(p).start()

    def extra_finish(p):
        @pl.when(helps)
        def _():
            e_copy(p).wait()
            eacc[p] += erecv[p]
            e_move(p).start()

    for j in range(ahead):
        send_own(j)
    for dz in range(1, lines):
        zz = (z + dz) % lines

        @pl.when(~is_end)
        def _():
            f_recv(zz).wait_recv()
            gather_start(0, zz)
    for j in range(ahead, chunks):
        for d in range(1, cols):
            d_send(j, d).start()

    @pl.when(helps)
    def _():
        f_own_end.wait()
        gather_start(1, z)
        for dz in range(1, lines):
            zz = (z + dz) % lines

            @pl.when(zz != end)
            def _():
                f_recv_end(zz).wait_recv()
                f_relay(zz).start()
                gather_start(1, zz)

    @pl.when(is_end)
    def _():
        for dz in range(1, lines):
            zz = (z + dz) % lines
            f_recv(zz).wait_recv()
            gather_start(0, zz)

    finished = 0
    e_finished = 0
    for i in range(chunks):
        if i + ahead < chunks:
            send_own(i + ahead)
        relay(i)
        if i == 0:
            for zz in range(lines):
                gather_forward(0, zz)
            for zz in range(lines):
                gather_end(0, zz)
        if i == min(2, chunks - 1):
            for step in (gather_forward, gather_end):
                for zz in range(lines):
                    @pl.when(helps & (zz != end))
                    def _():
                        step(1, zz)
        if i in part:
            extra(part.index(i))
        multiply(i)
        if e_finished < len(part) and part[e_finished] + E_LAG <= i:
            extra_finish(e_finished)
            e_finished += 1
        if i >= LAG:
            finish(finished)
            finished += 1
    while e_finished < len(part):
        extra_finish(e_finished)
        e_finished += 1
    while finished < chunks:
        finish(finished)
        finished += 1
    for p, j in enumerate(part):
        @pl.when(is_end)
        def _():
            e_move(p).wait_recv()
            acc[j] += eland[p]
            out_copy(j).start()

    for j in range(chunks):
        out_copy(j).wait()
        for d in range(1, cols):
            d_send(j, d).wait_send()
        for d in range(lines):
            @pl.when((z - d >= 0) & (z < most(j)))
            def _():
                z_right(j, z - d).wait_send()

            @pl.when((z + d < lines) & (z > least(j)))
            def _():
                z_left(j, z + d).wait_send()
    for dz in range(1, lines):
        f_send((z + dz) % lines).wait_send()
    for zz in range(lines):
        gather_drain(0, zz)

        @pl.when(helps & (zz != end))
        def _():
            gather_drain(1, zz)

            @pl.when(zz != z)
            def _():
                f_relay(zz).wait_send()
    for p in range(len(part)):
        @pl.when(helps)
        def _():
            e_move(p).wait_send()


def fused(row_count, cols, features, cotangent):
    lines = row_count // 2
    tok = features.shape[0]
    rows = features.shape[1] // lines
    width = cotangent.shape[1] // cols
    chunks = width // CHUNK
    part = partial_chunks(chunks)
    tokens = tok * cols * lines
    half = rows // 2
    parts = max(len(part), 1)
    dma = pltpu.SemaphoreType.DMA
    whole = pltpu.VMEM((chunks, half, CHUNK), jnp.float32)
    some = pltpu.VMEM((parts, half, CHUNK), jnp.float32)
    return pl.pallas_call(
        functools.partial(kernel, lines, cols, part),
        out_shape=jax.ShapeDtypeStruct((half, width), jnp.float32),
        in_specs=[pl.BlockSpec(memory_space=pl.ANY)] * 2,
        out_specs=pl.BlockSpec(memory_space=pl.ANY),
        scratch_shapes=[
            pltpu.VMEM((tokens, rows), jnp.bfloat16),
            pltpu.VMEM((tokens, rows), jnp.bfloat16),
            pltpu.VMEM((chunks, tokens, CHUNK), jnp.bfloat16),
            whole, whole, whole, some, some, some, some,
            dma((2,)), dma((chunks,)),
            dma((lines,)), dma((lines,)), dma((lines,)), dma((lines,)),
            dma((2, lines, cols)), dma((2, lines, cols)),
            dma((2, lines, cols)), dma((2, lines, cols)),
            dma((chunks, cols)), dma((chunks, cols)),
            dma((chunks, lines)), dma((chunks, lines)), dma((chunks, lines)),
            dma((chunks,)), dma((chunks,)),
            dma((parts,)), dma((parts,)), dma((parts,)), dma((parts,)),
            dma((chunks,)),
        ],
        compiler_params=pltpu.CompilerParams(
            collective_id=0, has_side_effects=True, vmem_limit_bytes=VMEM_MOST
        ),
    )(features, cotangent)


def fits(row_count, cols, features, cotangent):
    if row_count % 2 or cotangent.shape[1] % (cols * CHUNK):
        return False
    if features.shape[1] % (row_count * 128):
        return False
    lines = row_count // 2
    tokens = features.shape[0] * cols * lines
    rows = features.shape[1] // lines
    width = cotangent.shape[1] // cols
    held = 2 * tokens * (2 * rows + width) + 14 * rows * width
    return lines > 3 and cols % 2 == 0 and held <= VMEM_MOST


def local(row_count, cols, features, cotangent):
    if fits(row_count, cols, features, cotangent):
        return fused(row_count, cols, features, cotangent)
    return plain(features, cotangent)


def solution(mesh):
    placed = (P(("row", "col"), None), P(("row", "col"), None))
    body = functools.partial(local, mesh.shape["row"], mesh.shape["col"])
    return jax.shard_map(
        body, mesh=mesh, in_specs=placed, out_specs=P("row", "col"), check_vma=False
    )
```

profile of v0, /device:TPU:9, one launch (start us, length us, event | category | flops | bytes accessed | tf_op | source)
XLA Modules:
  0.0 252.7 jit_solution(14093172978017302154)
XLA Ops:
  0.0 248.0 %shard_map.28 = f32[512,2048]{1,0:T(8,128)} custom-call(bf16[192,4096]{1,0:T(8,128)(2,1)} %feat.1, bf16[192,8192]{1,0:T(8,128)(2,1)} %cot.1), custom_call_target="tpu_custom_call" | custom-call | tf_op jit(solution)/shard_map/pallas_call | solution.py:420
  248.0 4.7 %copy.4 = f32[512,2048]{1,0:T(8,128)} copy(f32[512,2048]{1,0:T(8,128)} %shard_map.28) | data formatting | bytes 8388608
where the time goes:
time: 257 us; the launch traced here: 253 us
  Pallas kernels  248 us (96%)
  local copies, waits for them, and re-layouts  4.7 us (2%)
    pallas_call x1, Pallas kernels, fused(): pl.pallas_call(functools.partial(kernel, lines, cols, part), out_shape=ja...  248 us

commit v1 on v0

v1 whole, which is shorter than its diff:
```python
import functools

import jax
import jax.numpy as jnp
from jax import lax
from jax.experimental import pallas as pl
from jax.experimental.pallas import tpu as pltpu
from jax.sharding import PartitionSpec as P

MESH = pl.DeviceIdType.MESH
CHUNK = 512
STRIP = 32
PAD = 16
PEAK = 181.0
VMEM_MOST = 60 * 1024 * 1024


def tokens_product(left, right):
    return lax.dot_general(
        left, right, (((0,), (0,)), ((), ())), preferred_element_type=jnp.float32
    )


def plain(features, cotangent):
    row_count = lax.axis_size("row")
    width_in = features.shape[1]
    local_rows = width_in // row_count
    columns = lax.all_to_all(cotangent, "col", split_axis=1, concat_axis=0, tiled=True)
    tok_local = features.shape[0]
    exchanged = lax.all_to_all(features, "row", split_axis=1, concat_axis=0, tiled=True)
    stacked = exchanged.reshape(row_count, tok_local, local_rows)
    gathered = lax.all_gather(stacked, "col", axis=1, tiled=True)
    all_tokens = gathered.reshape(-1, local_rows)
    return tokens_product(all_tokens, lax.all_gather(columns, "row", axis=0, tiled=True))


def encode(src, dst):
    rows, width = src.shape

    def strip(s):
        return pl.ds(pl.multiple_of(s * STRIP, STRIP), STRIP)

    top = lax.fori_loop(
        0, rows // STRIP, lambda s, m: jnp.maximum(m, jnp.abs(src[strip(s), :])),
        jnp.zeros((STRIP, width), jnp.float32),
    )
    top = jnp.max(top, axis=0, keepdims=True)
    undo = (jnp.maximum(top, 1e-30) * (1.0 / PEAK)).astype(jnp.bfloat16)
    dst[pl.ds(rows, PAD), :] = jnp.broadcast_to(undo, (PAD, width))
    scale = 1.0 / undo.astype(jnp.float32)

    @pl.loop(0, rows // STRIP)
    def _(s):
        t = src[strip(s), :] * scale
        u = t * t
        u = u * u
        u = u * u
        u = u * u
        dst[strip(s), :] = jnp.where(t < 0, -u, u).astype(jnp.bfloat16)


def decode_add(src, into):
    rows = into.shape[0]
    undo = src[pl.ds(rows, PAD), :].astype(jnp.float32)[:1]

    @pl.loop(0, rows // STRIP)
    def _(s):
        span = pl.ds(pl.multiple_of(s * STRIP, STRIP), STRIP)
        b = src[span, :].astype(jnp.float32)
        root = lax.rsqrt(jnp.maximum(jnp.abs(b), 1e-37))
        most = lax.rsqrt(lax.rsqrt(lax.rsqrt(root)))
        into[span, :] += (b * root) * root * most * undo


def kernel(
    lines, cols, feat, cot, out,
    fall, dall, tmp, ysend, yrecv, acc, msend, mrecv,
    fl, fz_s, fz_r, fx_s, fx_r, fm_s, fm_r,
    dl, dx_s, dx_r, dz_s, dz_r, y_s, y_r, m_s, m_r, o_s,
):
    row = lax.axis_index("row")
    col = lax.axis_index("col")
    z, y = row // 2, row % 2
    here = z % 2
    near = z + 1 - 2 * here
    far = lines - 1 - z
    tok = feat.shape[0]
    rows = fall.shape[2]
    half = rows // 2
    chunks = dall.shape[0]
    width = chunks * CHUNK

    def at_row(zz, yy):
        return {"row": zz * 2 + yy, "col": col}

    def at_col(d):
        return {"row": row, "col": (col + d) % cols}

    pair, mirror, partner = at_row(near, y), at_row(far, y), at_row(z, 1 - y)
    across = 2
    mate_col = col + 1 - 2 * (col % 2)
    mate = {"row": row, "col": mate_col}

    def remote(src, dst, s, r, dev):
        return pltpu.make_async_remote_copy(
            src_ref=src, dst_ref=dst, send_sem=s, recv_sem=r,
            device_id=dev, device_id_type=MESH,
        )

    barrier = pltpu.get_barrier_semaphore()
    others = [pair, mirror, partner] + [at_col(d) for d in range(1, cols)]
    for dev in others:
        pl.semaphore_signal(barrier, inc=1, device_id=dev, device_id_type=MESH)
    pl.semaphore_wait(barrier, len(others))

    def slot(plane, c):
        return pl.ds(pl.multiple_of((plane * cols + c) * tok, tok), tok)

    def f_cols(zz):
        return feat.at[:, pl.ds(pl.multiple_of(zz * rows, rows), rows)]

    def wanted(zz, g):
        return lines - 1 - zz if g == 0 else zz

    def f_own(g):
        return pltpu.make_async_copy(f_cols(wanted(z, g)), fall.at[g, slot(here, col)], fl.at[g])

    def f_pair(g):
        return remote(
            f_cols(wanted(near, g)), fall.at[g, slot(here, col)], fz_s.at[g], fz_r.at[g], pair
        )

    def f_block(g, other, c):
        return fall.at[g, slot(1 - here if other else here, c)]

    def f_across(g, other):
        block = f_block(g, other, col)
        src = block if other else f_cols(wanted(z, g))
        return remote(src, block, fx_s.at[g, other], fx_r.at[g, other], at_col(across))

    def f_mate(g, other, k):
        block = f_block(g, other, (col + across * k) % cols)
        src = f_cols(wanted(z, g)) if not other and not k else block
        return remote(src, block, fm_s.at[g, other, k], fm_r.at[g, other, k], mate)

    def d_cols(cc, j):
        return cot.at[:, pl.ds(pl.multiple_of(cc * width + j * CHUNK, CHUNK), CHUNK)]

    def d_own(j):
        return pltpu.make_async_copy(d_cols(col, j), dall.at[j, slot(here, col)], dl.at[j])

    def d_send(j, d):
        return remote(
            d_cols((col + d) % cols, j), dall.at[j, slot(here, col)],
            dx_s.at[j, d], dx_r.at[j, d], at_col(d),
        )

    def d_pair(j, d):
        block = dall.at[j, slot(here, (col + cols - d) % cols)]
        return remote(
            d_cols(col, j) if d == 0 else block, block, dz_s.at[j, d], dz_r.at[j, d], pair
        )

    def y_copy(g, j):
        return remote(ysend.at[g, j], yrecv.at[g, j], y_s.at[g, j], y_r.at[g, j], partner)

    def m_copy(j):
        return remote(msend.at[j], mrecv.at[j], m_s.at[j], m_r.at[j], mirror)

    def out_copy(j):
        return pltpu.make_async_copy(acc.at[1, j], out.at[:, pl.ds(j * CHUNK, CHUNK)], o_s.at[j])

    def d_issue(j):
        d_own(j).start()
        d_pair(j, 0).start()
        for d in (1, 3, 2):
            d_send(j, d).start()

    def d_relay(j):
        for d in (1, 3, 2):
            d_send(j, d).wait_recv()
            d_pair(j, d).start()

    def f_issue(g):
        f_pair(g).start()
        f_across(g, 0).start()
        f_mate(g, 0, 0).start()
        f_own(g).start()

    def f_relay(g):
        f_across(g, 0).wait_recv()
        f_mate(g, 0, 1).start()
        f_pair(g).wait_recv()
        f_across(g, 1).start()
        f_mate(g, 1, 0).start()

    def f_end(g):
        f_across(g, 1).wait_recv()
        f_mate(g, 1, 1).start()
        f_own(g).wait()
        for other in range(2):
            for k in range(2):
                f_mate(g, other, k).wait_recv()

    def d_end(j):
        d_own(j).wait()
        for d in range(cols):
            d_pair(j, d).wait_recv()

    def columns_of(which):
        return pl.ds(pl.multiple_of(which * half, half), half)

    def multiply(g, j):
        tmp[...] = tokens_product(fall[g, :, columns_of(1 - y)], dall[j])
        encode(tmp, ysend.at[g, j])
        y_copy(g, j).start()
        acc[g, j] = tokens_product(fall[g, :, columns_of(y)], dall[j])

    def finish(g, j):
        y_copy(g, j).wait_recv()
        decode_add(yrecv.at[g, j], acc.at[g, j])
        if g == 0:
            encode(acc.at[0, j], msend.at[j])
            m_copy(j).start()

    f_issue(0)
    d_issue(0)
    f_relay(0)
    d_relay(0)
    f_issue(1)
    d_issue(1)
    f_end(0)
    for i in range(chunks):
        if i + 1 < chunks:
            d_relay(i + 1)
        if i + 2 < chunks:
            d_issue(i + 2)
        d_end(i)
        multiply(0, i)
        if i == 0:
            f_relay(1)
            f_end(1)
        multiply(1, i)
        if i >= 1:
            finish(1, i - 1)
        finish(0, i)
    finish(1, chunks - 1)
    for j in range(chunks):
        m_copy(j).wait_recv()
        decode_add(mrecv.at[j], acc.at[1, j])
        out_copy(j).start()

    for g in range(2):
        f_pair(g).wait_send()
        for other in range(2):
            f_across(g, other).wait_send()
            for k in range(2):
                f_mate(g, other, k).wait_send()
    for j in range(chunks):
        for d in range(cols):
            d_pair(j, d).wait_send()
        for d in range(1, cols):
            d_send(j, d).wait_send()
        for g in range(2):
            y_copy(g, j).wait_send()
        m_copy(j).wait_send()
        out_copy(j).wait()


def sizes(row_count, cols, features, cotangent):
    lines = row_count // 2
    tokens = 2 * features.shape[0] * cols
    rows = features.shape[1] // lines
    width = cotangent.shape[1] // cols
    return lines, tokens, rows, width


def fused(row_count, cols, features, cotangent):
    lines, tokens, rows, width = sizes(row_count, cols, features, cotangent)
    chunks = width // CHUNK
    half = rows // 2
    dma = pltpu.SemaphoreType.DMA
    coded = pltpu.VMEM((2, chunks, half + PAD, CHUNK), jnp.bfloat16)
    moved = pltpu.VMEM((chunks, half + PAD, CHUNK), jnp.bfloat16)
    return pl.pallas_call(
        functools.partial(kernel, lines, cols),
        out_shape=jax.ShapeDtypeStruct((half, width), jnp.float32),
        in_specs=[pl.BlockSpec(memory_space=pl.ANY)] * 2,
        out_specs=pl.BlockSpec(memory_space=pl.ANY),
        scratch_shapes=[
            pltpu.VMEM((2, tokens, rows), jnp.bfloat16),
            pltpu.VMEM((chunks, tokens, CHUNK), jnp.bfloat16),
            pltpu.VMEM((half, CHUNK), jnp.float32),
            coded, coded,
            pltpu.VMEM((2, chunks, half, CHUNK), jnp.float32),
            moved, moved,
            dma((2,)), dma((2,)), dma((2,)),
            dma((2, 2)), dma((2, 2)), dma((2, 2, 2)), dma((2, 2, 2)),
            dma((chunks,)), dma((chunks, cols)), dma((chunks, cols)),
            dma((chunks, cols)), dma((chunks, cols)),
            dma((2, chunks)), dma((2, chunks)), dma((chunks,)), dma((chunks,)),
            dma((chunks,)),
        ],
        compiler_params=pltpu.CompilerParams(
            collective_id=0, has_side_effects=True, vmem_limit_bytes=VMEM_MOST
        ),
    )(features, cotangent)


def fits(row_count, cols, features, cotangent):
    if row_count != 8 or cols != 4 or cotangent.shape[1] % (cols * CHUNK):
        return False
    if features.shape[1] % (row_count * 128) or features.shape[0] % 16:
        return False
    lines, tokens, rows, width = sizes(row_count, cols, features, cotangent)
    held = 2 * tokens * (2 * rows + width) + 11 * rows * width + 4 * rows * CHUNK
    return held <= VMEM_MOST


def local(row_count, cols, features, cotangent):
    if fits(row_count, cols, features, cotangent):
        return fused(row_count, cols, features, cotangent)
    return plain(features, cotangent)


def solution(mesh):
    placed = (P(("row", "col"), None), P(("row", "col"), None))
    body = functools.partial(local, mesh.shape["row"], mesh.shape["col"])
    return jax.shard_map(
        body, mesh=mesh, in_specs=placed, out_specs=P("row", "col"), check_vma=False
    )
```

time: 257 us -> 174 us (0.68); the launches traced: 253 us -> 174 us
  Pallas kernels: 248 us -> 169 us
    pallas_call x1, Pallas kernels: 248 us -> 169 us  [fused(): pl.pallas_call(functools.partial(kernel, lines, cols), out_shape=jax.Shap...]
where the time goes in v1:
time: 174 us
  Pallas kernels  169 us (97%)
  local copies, waits for them, and re-layouts  4.7 us (3%)
    pallas_call x1, Pallas kernels, fused(): pl.pallas_call(functools.partial(kernel, lines, cols), out_shape=jax.Shap...  169 us
    unnamed x1, local copies, waits for them, and re-layouts  4.7 us

profile of v1, /device:TPU:9, one launch (start us, length us, event | category | flops | bytes accessed | tf_op | source)
XLA Modules:
  0.0 174.1 jit_solution(11155486954723175508)
XLA Ops:
  0.0 169.4 %shard_map.28 = f32[512,2048]{1,0:T(8,128)} custom-call(bf16[192,4096]{1,0:T(8,128)(2,1)} %feat.1, bf16[192,8192]{1,0:T(8,128)(2,1)} %cot.1), custom_call_target="tpu_custom_call" | custom-call | tf_op jit(solution)/shard_map/pallas_call | solution.py:285
  169.4 4.7 %copy.4 = f32[512,2048]{1,0:T(8,128)} copy(f32[512,2048]{1,0:T(8,128)} %shard_map.28) | data formatting | bytes 8388608

commit v2 on v1

v2 whole, which is shorter than its diff:
```python
import functools

import jax
import jax.numpy as jnp
from jax import lax
from jax.experimental import pallas as pl
from jax.experimental.pallas import tpu as pltpu
from jax.sharding import PartitionSpec as P

MESH = pl.DeviceIdType.MESH
CHUNKS = 8
STRIP = 32
PAD = 16
PEAK = 181.0
VMEM_MOST = 60 * 1024 * 1024


ORDER = (
    ("F", 0), ("D", 0), ("F", 2), ("relay", 0), ("D", 1), ("forward", "F", 0), ("relay", 1),
    ("D", 2), ("relay_across", 0), ("relay", 2), ("D", 3), ("forward", "F", 2), ("relay", 3),
    ("P", 0), ("relay_across", 1), ("D", 4), ("relay_across", 2), ("relay", 4), ("D", 5),
    ("relay_across", 3), ("relay", 5), ("D", 6), ("forward", "P", 0), ("give", 0, 0),
    ("relay", 6), ("P", 2), ("relay_across", 4), ("give", 0, 1), ("D", 7), ("relay_across", 5),
    ("relay", 7), ("give", 0, 2), ("F", 1), ("relay_across", 6), ("F", 3), ("forward", "P", 2),
    ("keep", 0, 0), ("finish", 0, 0), ("give", 0, 3), ("relay_across", 7), ("keep", 0, 1),
    ("finish", 0, 1), ("keep", 0, 2), ("finish", 0, 2), ("forward", "F", 1), ("keep", 0, 3),
    ("finish", 0, 3), ("forward", "F", 3), ("give", 0, 4), ("keep", 0, 4), ("give", 0, 5),
    ("keep", 0, 5), ("finish", 0, 4), ("P", 1), ("finish", 0, 5), ("give", 0, 6), ("keep", 0, 6),
    ("forward", "P", 1), ("give", 1, 0), ("P", 3), ("give", 1, 1), ("give", 1, 2),
    ("give", 1, 3), ("finish", 0, 6), ("give", 1, 4), ("forward", "P", 3), ("give", 1, 5),
    ("keep", 1, 0), ("keep", 1, 1), ("keep", 1, 2), ("keep", 1, 3), ("keep", 1, 4),
    ("keep", 1, 5), ("keep", 1, 6), ("give", 0, 7), ("keep", 0, 7), ("keep", 1, 7),
    ("finish", 1, 0), ("finish", 1, 1), ("give", 1, 6), ("finish", 1, 2), ("give", 1, 7),
    ("last", 0), ("last", 1), ("finish", 1, 3), ("last", 2), ("finish", 1, 4), ("last", 3),
    ("finish", 1, 5), ("last", 4), ("finish", 0, 7), ("last", 5), ("finish", 1, 6),
    ("finish", 1, 7), ("last", 6), ("last", 7),
)


def tokens_product(left, right):
    return lax.dot_general(
        left, right, (((0,), (0,)), ((), ())), preferred_element_type=jnp.float32
    )


def plain(features, cotangent):
    row_count = lax.axis_size("row")
    width_in = features.shape[1]
    local_rows = width_in // row_count
    columns = lax.all_to_all(cotangent, "col", split_axis=1, concat_axis=0, tiled=True)
    tok_local = features.shape[0]
    exchanged = lax.all_to_all(features, "row", split_axis=1, concat_axis=0, tiled=True)
    stacked = exchanged.reshape(row_count, tok_local, local_rows)
    gathered = lax.all_gather(stacked, "col", axis=1, tiled=True)
    all_tokens = gathered.reshape(-1, local_rows)
    return tokens_product(all_tokens, lax.all_gather(columns, "row", axis=0, tiled=True))


def encode(src, dst):
    rows, width = src.shape

    def strip(s):
        return pl.ds(pl.multiple_of(s * STRIP, STRIP), STRIP)

    top = lax.fori_loop(
        0, rows // STRIP, lambda s, m: jnp.maximum(m, jnp.abs(src[strip(s), :])),
        jnp.zeros((STRIP, width), jnp.float32),
    )
    top = jnp.max(top, axis=0, keepdims=True)
    undo = (jnp.maximum(top, 1e-30) * (1.0 / PEAK)).astype(jnp.bfloat16)
    dst[pl.ds(rows, PAD), :] = jnp.broadcast_to(undo, (PAD, width))
    scale = 1.0 / undo.astype(jnp.float32)

    @pl.loop(0, rows // STRIP)
    def _(s):
        t = src[strip(s), :] * scale
        u = t * t
        u = u * u
        u = u * u
        u = u * u
        dst[strip(s), :] = jnp.where(t < 0, -u, u).astype(jnp.bfloat16)


def decode_add(src, into):
    rows = into.shape[0]
    undo = src[pl.ds(rows, PAD), :].astype(jnp.float32)[:1]

    @pl.loop(0, rows // STRIP)
    def _(s):
        span = pl.ds(pl.multiple_of(s * STRIP, STRIP), STRIP)
        b = src[span, :].astype(jnp.float32)
        root = lax.rsqrt(jnp.maximum(jnp.abs(b), 1e-37))
        most = lax.rsqrt(lax.rsqrt(lax.rsqrt(root)))
        into[span, :] += (b * root) * root * most * undo


def kernel(
    lines, cols, feat, cot, out,
    fall, dall, tmp, ysend, yrecv, acc, msend, mrecv,
    fl, fz_s, fz_r, fx_s, fx_r, fm_s, fm_r,
    dl, dx_s, dx_r, dz_s, dz_r, y_s, y_r, m_s, m_r, o_s,
):
    row = lax.axis_index("row")
    col = lax.axis_index("col")
    z, y = row // 2, row % 2
    here = z % 2
    near = z + 1 - 2 * here
    far = lines - 1 - z
    tok = feat.shape[0]
    half = fall.shape[2]
    chunks, _, chunk = dall.shape
    width = chunks * chunk

    def at_row(zz, yy):
        return {"row": zz * 2 + yy, "col": col}

    pair, mirror, partner = at_row(near, y), at_row(far, y), at_row(z, 1 - y)
    mate_col = col + 1 - 2 * (col % 2)
    col_of = (col, mate_col, (col + 2) % cols, (mate_col + 2) % cols)
    MATE, ACROSS = 1, 2

    def at_col(k):
        return {"row": row, "col": col_of[k]}

    def remote(src, dst, s, r, dev):
        return pltpu.make_async_remote_copy(
            src_ref=src, dst_ref=dst, send_sem=s, recv_sem=r,
            device_id=dev, device_id_type=MESH,
        )

    barrier = pltpu.get_barrier_semaphore()
    others = [pair, mirror, partner] + [at_col(k) for k in range(1, cols)]
    for dev in others:
        pl.semaphore_signal(barrier, inc=1, device_id=dev, device_id_type=MESH)
    pl.semaphore_wait(barrier, len(others))

    def slot(plane, c):
        return pl.ds(pl.multiple_of((plane * cols + c) * tok, tok), tok)

    def f_cols(zz, q):
        wanted = lines - 1 - zz if q % 2 == 0 else zz
        yy = 1 - y if q < 2 else y
        return feat.at[:, pl.ds(pl.multiple_of((wanted * 2 + yy) * half, half), half)]

    def f_own(q):
        return pltpu.make_async_copy(f_cols(z, q), fall.at[q, slot(here, col)], fl.at[q])

    def f_pair(q):
        return remote(f_cols(near, q), fall.at[q, slot(here, col)], fz_s.at[q], fz_r.at[q], pair)

    def f_block(q, other, k):
        return fall.at[q, slot(1 - here if other else here, col_of[k])]

    def f_across(q, other):
        block = f_block(q, other, 0)
        src = block if other else f_cols(z, q)
        return remote(src, block, fx_s.at[q, other], fx_r.at[q, other], at_col(ACROSS))

    def f_mate(q, other, k):
        block = f_block(q, other, ACROSS * k)
        src = f_cols(z, q) if not other and not k else block
        return remote(src, block, fm_s.at[q, other, k], fm_r.at[q, other, k], at_col(MATE))

    def d_cols(cc, j):
        return cot.at[:, pl.ds(pl.multiple_of(cc * width + j * chunk, chunk), chunk)]

    def d_own(j):
        return pltpu.make_async_copy(d_cols(col, j), dall.at[j, slot(here, col)], dl.at[j])

    def d_send(j, k):
        return remote(
            d_cols(col_of[k], j), dall.at[j, slot(here, col)],
            dx_s.at[j, k], dx_r.at[j, k], at_col(k),
        )

    def d_pair(j, k):
        block = dall.at[j, slot(here, col_of[k])]
        return remote(
            block if k else d_cols(col, j), block, dz_s.at[j, k], dz_r.at[j, k], pair
        )

    def y_copy(g, j):
        return remote(ysend.at[g, j], yrecv.at[g, j], y_s.at[g, j], y_r.at[g, j], partner)

    def m_copy(j):
        return remote(msend.at[j], mrecv.at[j], m_s.at[j], m_r.at[j], mirror)

    def out_copy(j):
        return pltpu.make_async_copy(acc.at[1, j], out.at[:, pl.ds(j * chunk, chunk)], o_s.at[j])

    ready = set()

    def once(key):
        new = key not in ready
        ready.add(key)
        return new

    def arrive(q, j):
        if once(("F", q)):
            f_own(q).wait()
            for other in range(2):
                for k in range(2):
                    f_mate(q, other, k).wait_recv()
        if once(("D", j)):
            d_own(j).wait()
            for k in range(cols):
                d_pair(j, k).wait_recv()

    def do_F(q):
        f_pair(q).start()
        f_across(q, 0).start()
        f_mate(q, 0, 0).start()
        f_own(q).start()

    def do_P(q):
        f_pair(q).wait_recv()
        f_across(q, 1).start()
        f_mate(q, 1, 0).start()

    def do_D(j):
        d_pair(j, 0).start()
        for k in (2, 3, 1):
            d_send(j, k).start()
        d_own(j).start()

    def do_forward(kind, q):
        other = 1 if kind == "P" else 0
        f_across(q, other).wait_recv()
        f_mate(q, other, 1).start()

    def do_relay(j):
        d_send(j, MATE).wait_recv()
        d_pair(j, MATE).start()

    def do_relay_across(j):
        for k in (2, 3):
            d_send(j, k).wait_recv()
            d_pair(j, k).start()

    def do_give(g, j):
        arrive(g, j)
        tmp[...] = tokens_product(fall[g], dall[j])
        encode(tmp, ysend.at[g, j])
        y_copy(g, j).start()

    def do_keep(g, j):
        arrive(2 + g, j)
        acc[g, j] = tokens_product(fall[2 + g], dall[j])

    def do_finish(g, j):
        y_copy(g, j).wait_recv()
        decode_add(yrecv.at[g, j], acc.at[g, j])
        if g == 0:
            encode(acc.at[0, j], msend.at[j])
            m_copy(j).start()

    def do_last(j):
        m_copy(j).wait_recv()
        decode_add(mrecv.at[j], acc.at[1, j])
        out_copy(j).start()

    run = {
        "F": do_F, "P": do_P, "D": do_D, "forward": do_forward, "relay": do_relay,
        "relay_across": do_relay_across, "give": do_give, "keep": do_keep,
        "finish": do_finish, "last": do_last,
    }
    for name, *which in ORDER:
        with jax.named_scope(name + "".join(str(w) for w in which)):
            run[name](*which)

    for q in range(4):
        f_pair(q).wait_send()
        for other in range(2):
            f_across(q, other).wait_send()
            for k in range(2):
                f_mate(q, other, k).wait_send()
    for j in range(chunks):
        for k in range(cols):
            d_pair(j, k).wait_send()
        for k in range(1, cols):
            d_send(j, k).wait_send()
        for g in range(2):
            y_copy(g, j).wait_send()
        m_copy(j).wait_send()
        out_copy(j).wait()


def sizes(row_count, cols, features, cotangent):
    lines = row_count // 2
    tokens = 2 * features.shape[0] * cols
    rows = features.shape[1] // lines
    width = cotangent.shape[1] // cols
    return lines, tokens, rows, width


def fused(row_count, cols, features, cotangent):
    lines, tokens, rows, width = sizes(row_count, cols, features, cotangent)
    chunks, chunk = CHUNKS, width // CHUNKS
    half = rows // 2
    dma = pltpu.SemaphoreType.DMA
    coded = pltpu.VMEM((2, chunks, half + PAD, chunk), jnp.bfloat16)
    moved = pltpu.VMEM((chunks, half + PAD, chunk), jnp.bfloat16)
    return pl.pallas_call(
        functools.partial(kernel, lines, cols),
        out_shape=jax.ShapeDtypeStruct((half, width), jnp.float32),
        in_specs=[pl.BlockSpec(memory_space=pl.ANY)] * 2,
        out_specs=pl.BlockSpec(memory_space=pl.ANY),
        scratch_shapes=[
            pltpu.VMEM((4, tokens, half), jnp.bfloat16),
            pltpu.VMEM((chunks, tokens, chunk), jnp.bfloat16),
            pltpu.VMEM((half, chunk), jnp.float32),
            coded, coded,
            pltpu.VMEM((2, chunks, half, chunk), jnp.float32),
            moved, moved,
            dma((4,)), dma((4,)), dma((4,)),
            dma((4, 2)), dma((4, 2)), dma((4, 2, 2)), dma((4, 2, 2)),
            dma((chunks,)), dma((chunks, cols)), dma((chunks, cols)),
            dma((chunks, cols)), dma((chunks, cols)),
            dma((2, chunks)), dma((2, chunks)), dma((chunks,)), dma((chunks,)),
            dma((chunks,)),
        ],
        compiler_params=pltpu.CompilerParams(
            collective_id=0, has_side_effects=True, vmem_limit_bytes=VMEM_MOST
        ),
    )(features, cotangent)


def fits(row_count, cols, features, cotangent):
    if row_count != 8 or cols != 4 or cotangent.shape[1] % (cols * CHUNKS * 128):
        return False
    if features.shape[1] % (row_count * 128) or features.shape[0] % 16:
        return False
    lines, tokens, rows, width = sizes(row_count, cols, features, cotangent)
    held = 2 * tokens * (2 * rows + width) + 11 * rows * width + 4 * rows * width // CHUNKS
    return held <= VMEM_MOST


def local(row_count, cols, features, cotangent):
    if fits(row_count, cols, features, cotangent):
        return fused(row_count, cols, features, cotangent)
    return plain(features, cotangent)


def solution(mesh):
    placed = (P(("row", "col"), None), P(("row", "col"), None))
    body = functools.partial(local, mesh.shape["row"], mesh.shape["col"])
    return jax.shard_map(
        body, mesh=mesh, in_specs=placed, out_specs=P("row", "col"), check_vma=False
    )
```

time: 174 us -> 157 us (0.902)
  Pallas kernels: 169 us -> 153 us
    pallas_call x1, Pallas kernels: 169 us -> 153 us  [fused(): pl.pallas_call(functools.partial(kernel, lines, cols), out_shape=jax.Shap...]
where the time goes in v2:
time: 157 us
  Pallas kernels  153 us (97%)
  local copies, waits for them, and re-layouts  4.7 us (3%)
    pallas_call x1, Pallas kernels, fused(): pl.pallas_call(functools.partial(kernel, lines, cols), out_shape=jax.Shap...  153 us
    unnamed x1, local copies, waits for them, and re-layouts  4.7 us

profile of v2, /device:TPU:9, one launch (start us, length us, event | category | flops | bytes accessed | tf_op | source)
XLA Modules:
  0.0 157.2 jit_solution(3933374050782888869)
XLA Ops:
  0.0 152.5 %shard_map.28 = f32[512,2048]{1,0:T(8,128)} custom-call(bf16[192,4096]{1,0:T(8,128)(2,1)} %feat.1, bf16[192,8192]{1,0:T(8,128)(2,1)} %cot.1), custom_call_target="tpu_custom_call" | custom-call | tf_op jit(solution)/shard_map/pallas_call | solution.py:303
  152.5 4.7 %copy.4 = f32[512,2048]{1,0:T(8,128)} copy(f32[512,2048]{1,0:T(8,128)} %shard_map.28) | data formatting | bytes 8388608

commit v3 on v2

--- a/solution.py
+++ b/solution.py
@@ -16,24 +16,25 @@
 
 
 ORDER = (
-    ("F", 0), ("D", 0), ("F", 2), ("relay", 0), ("D", 1), ("forward", "F", 0), ("relay", 1),
-    ("D", 2), ("relay_across", 0), ("relay", 2), ("D", 3), ("forward", "F", 2), ("relay", 3),
-    ("P", 0), ("relay_across", 1), ("D", 4), ("relay_across", 2), ("relay", 4), ("D", 5),
-    ("relay_across", 3), ("relay", 5), ("D", 6), ("forward", "P", 0), ("give", 0, 0),
-    ("relay", 6), ("P", 2), ("relay_across", 4), ("give", 0, 1), ("D", 7), ("relay_across", 5),
-    ("relay", 7), ("give", 0, 2), ("F", 1), ("relay_across", 6), ("F", 3), ("forward", "P", 2),
-    ("keep", 0, 0), ("finish", 0, 0), ("give", 0, 3), ("relay_across", 7), ("keep", 0, 1),
-    ("finish", 0, 1), ("keep", 0, 2), ("finish", 0, 2), ("forward", "F", 1), ("keep", 0, 3),
-    ("finish", 0, 3), ("forward", "F", 3), ("give", 0, 4), ("keep", 0, 4), ("give", 0, 5),
-    ("keep", 0, 5), ("finish", 0, 4), ("P", 1), ("finish", 0, 5), ("give", 0, 6), ("keep", 0, 6),
-    ("forward", "P", 1), ("give", 1, 0), ("P", 3), ("give", 1, 1), ("give", 1, 2),
-    ("give", 1, 3), ("finish", 0, 6), ("give", 1, 4), ("forward", "P", 3), ("give", 1, 5),
-    ("keep", 1, 0), ("keep", 1, 1), ("keep", 1, 2), ("keep", 1, 3), ("keep", 1, 4),
-    ("keep", 1, 5), ("keep", 1, 6), ("give", 0, 7), ("keep", 0, 7), ("keep", 1, 7),
-    ("finish", 1, 0), ("finish", 1, 1), ("give", 1, 6), ("finish", 1, 2), ("give", 1, 7),
-    ("last", 0), ("last", 1), ("finish", 1, 3), ("last", 2), ("finish", 1, 4), ("last", 3),
-    ("finish", 1, 5), ("last", 4), ("finish", 0, 7), ("last", 5), ("finish", 1, 6),
-    ("finish", 1, 7), ("last", 6), ("last", 7),
+    ("Z", 0), ("Z", 2), ("F", 0), ("D", 0), ("relay", 0), ("forward", "F", 0), ("P", 0),
+    ("relay_across", 0), ("D", 1), ("relay", 1), ("forward", "P", 0), ("D", 2), ("relay", 2),
+    ("give", 0, 0), ("relay_across", 1), ("F", 2), ("relay_across", 2), ("D", 3), ("relay", 3),
+    ("forward", "F", 2), ("F", 3), ("give", 0, 1), ("relay_across", 3), ("P", 2), ("give", 0, 2),
+    ("forward", "F", 3), ("D", 4), ("relay", 4), ("forward", "P", 2), ("D", 5), ("keep", 0, 0),
+    ("finish", 0, 0), ("relay", 5), ("keep", 0, 2), ("keep", 0, 3), ("give", 0, 3),
+    ("finish", 0, 2), ("relay_across", 4), ("D", 6), ("keep", 0, 1), ("finish", 0, 1),
+    ("relay_across", 5), ("relay", 6), ("F", 1), ("relay_across", 6), ("Z", 1), ("D", 7),
+    ("finish", 0, 3), ("relay", 7), ("give", 0, 4), ("forward", "F", 1), ("keep", 0, 4),
+    ("relay_across", 7), ("Z", 3), ("far", 0), ("far", 1), ("far", 2), ("far", 3),
+    ("give", 0, 5), ("keep", 0, 5), ("finish", 0, 4), ("far", 4), ("give", 0, 6), ("keep", 0, 6),
+    ("finish", 0, 5), ("far", 5), ("P", 1), ("finish", 0, 6), ("far", 6), ("forward", "P", 1),
+    ("give", 1, 0), ("give", 1, 1), ("give", 0, 7), ("keep", 0, 7), ("P", 3),
+    ("forward", "P", 3), ("give", 1, 7), ("keep", 1, 7), ("keep", 1, 5), ("keep", 1, 4),
+    ("keep", 1, 6), ("keep", 1, 1), ("give", 1, 2), ("finish", 0, 7), ("far", 7),
+    ("finish", 1, 1), ("last", 1), ("keep", 1, 0), ("finish", 1, 0), ("give", 1, 6), ("last", 0),
+    ("finish", 1, 7), ("keep", 1, 2), ("keep", 1, 3), ("give", 1, 4), ("finish", 1, 2),
+    ("last", 2), ("give", 1, 3), ("finish", 1, 6), ("give", 1, 5), ("finish", 1, 4), ("last", 4),
+    ("finish", 1, 3), ("last", 3), ("last", 6), ("finish", 1, 5), ("last", 5), ("last", 7),
 )
 
 
@@ -106,6 +107,7 @@
     here = z % 2
     near = z + 1 - 2 * here
     far = lines - 1 - z
+    inner = (z > 0) & (z < lines - 1)
     tok = feat.shape[0]
     half = fall.shape[2]
     chunks, _, chunk = dall.shape
@@ -206,8 +208,10 @@
             for k in range(cols):
                 d_pair(j, k).wait_recv()
 
+    def do_Z(q):
+        f_pair(q).start()
+
     def do_F(q):
-        f_pair(q).start()
         f_across(q, 0).start()
         f_mate(q, 0, 0).start()
         f_own(q).start()
@@ -252,6 +256,14 @@
         decode_add(yrecv.at[g, j], acc.at[g, j])
         if g == 0:
             encode(acc.at[0, j], msend.at[j])
+
+            @pl.when(inner)
+            def _():
+                m_copy(j).start()
+
+    def do_far(j):
+        @pl.when(~inner)
+        def _():
             m_copy(j).start()
 
     def do_last(j):
@@ -260,7 +272,7 @@
         out_copy(j).start()
 
     run = {
-        "F": do_F, "P": do_P, "D": do_D, "forward": do_forward, "relay": do_relay,
+        "Z": do_Z, "F": do_F, "P": do_P, "far": do_far, "D": do_D, "forward": do_forward, "relay": do_relay,
         "relay_across": do_relay_across, "give": do_give, "keep": do_keep,
         "finish": do_finish, "last": do_last,
     }

time: 157 us -> 150 us (0.955)
  Pallas kernels: 153 us -> 146 us
    pallas_call x1, Pallas kernels: 153 us -> 146 us  [fused(): pl.pallas_call(functools.partial(kernel, lines, cols), out_shape=jax.Shap...]
where the time goes in v3:
time: 150 us
  Pallas kernels  146 us (97%)
  local copies, waits for them, and re-layouts  4.7 us (3%)
    pallas_call x1, Pallas kernels, fused(): pl.pallas_call(functools.partial(kernel, lines, cols), out_shape=jax.Shap...  146 us
    unnamed x1, local copies, waits for them, and re-layouts  4.7 us

profile of v3, /device:TPU:9, one launch (start us, length us, event | category | flops | bytes accessed | tf_op | source)
XLA Modules:
  0.0 150.2 jit_solution(800397676852311344)
XLA Ops:
  0.0 145.5 %shard_map.28 = f32[512,2048]{1,0:T(8,128)} custom-call(bf16[192,4096]{1,0:T(8,128)(2,1)} %feat.1, bf16[192,8192]{1,0:T(8,128)(2,1)} %cot.1), custom_call_target="tpu_custom_call" | custom-call | tf_op jit(solution)/shard_map/pallas_call | solution.py:315
  145.5 4.7 %copy.4 = f32[512,2048]{1,0:T(8,128)} copy(f32[512,2048]{1,0:T(8,128)} %shard_map.28) | data formatting | bytes 8388608

commit v4 on v3

--- a/solution.py
+++ b/solution.py
@@ -8,33 +8,34 @@
 from jax.sharding import PartitionSpec as P
 
 MESH = pl.DeviceIdType.MESH
-CHUNKS = 8
+WIDTHS = (1, 1, 1, 1, 1, 1, 1, 1)
+PARTS = sum(WIDTHS)
 STRIP = 32
-PAD = 16
 PEAK = 181.0
-VMEM_MOST = 60 * 1024 * 1024
+VMEM_MOST = 58 * 1024 * 1024
 
 
 ORDER = (
     ("Z", 0), ("Z", 2), ("F", 0), ("D", 0), ("relay", 0), ("forward", "F", 0), ("P", 0),
     ("relay_across", 0), ("D", 1), ("relay", 1), ("forward", "P", 0), ("D", 2), ("relay", 2),
-    ("give", 0, 0), ("relay_across", 1), ("F", 2), ("relay_across", 2), ("D", 3), ("relay", 3),
-    ("forward", "F", 2), ("F", 3), ("give", 0, 1), ("relay_across", 3), ("P", 2), ("give", 0, 2),
-    ("forward", "F", 3), ("D", 4), ("relay", 4), ("forward", "P", 2), ("D", 5), ("keep", 0, 0),
-    ("finish", 0, 0), ("relay", 5), ("keep", 0, 2), ("keep", 0, 3), ("give", 0, 3),
-    ("finish", 0, 2), ("relay_across", 4), ("D", 6), ("keep", 0, 1), ("finish", 0, 1),
-    ("relay_across", 5), ("relay", 6), ("F", 1), ("relay_across", 6), ("Z", 1), ("D", 7),
-    ("finish", 0, 3), ("relay", 7), ("give", 0, 4), ("forward", "F", 1), ("keep", 0, 4),
-    ("relay_across", 7), ("Z", 3), ("far", 0), ("far", 1), ("far", 2), ("far", 3),
-    ("give", 0, 5), ("keep", 0, 5), ("finish", 0, 4), ("far", 4), ("give", 0, 6), ("keep", 0, 6),
-    ("finish", 0, 5), ("far", 5), ("P", 1), ("finish", 0, 6), ("far", 6), ("forward", "P", 1),
-    ("give", 1, 0), ("give", 1, 1), ("give", 0, 7), ("keep", 0, 7), ("P", 3),
-    ("forward", "P", 3), ("give", 1, 7), ("keep", 1, 7), ("keep", 1, 5), ("keep", 1, 4),
-    ("keep", 1, 6), ("keep", 1, 1), ("give", 1, 2), ("finish", 0, 7), ("far", 7),
-    ("finish", 1, 1), ("last", 1), ("keep", 1, 0), ("finish", 1, 0), ("give", 1, 6), ("last", 0),
-    ("finish", 1, 7), ("keep", 1, 2), ("keep", 1, 3), ("give", 1, 4), ("finish", 1, 2),
-    ("last", 2), ("give", 1, 3), ("finish", 1, 6), ("give", 1, 5), ("finish", 1, 4), ("last", 4),
-    ("finish", 1, 3), ("last", 3), ("last", 6), ("finish", 1, 5), ("last", 5), ("last", 7),
+    ("give", 0, 0), ("relay_across", 1), ("D", 3), ("relay", 3), ("relay_across", 2), ("D", 4),
+    ("relay", 4), ("relay_across", 3), ("F", 2), ("give", 0, 1), ("relay_across", 4), ("P", 2),
+    ("forward", "F", 2), ("D", 5), ("relay", 5), ("give", 0, 2), ("forward", "P", 2), ("F", 3),
+    ("keep", 0, 2), ("keep", 0, 1), ("relay_across", 5), ("D", 6), ("finish", 0, 1),
+    ("keep", 0, 0), ("finish", 0, 0), ("relay", 6), ("forward", "F", 3), ("F", 1),
+    ("give", 0, 3), ("finish", 0, 2), ("keep", 0, 3), ("relay_across", 6), ("give", 0, 4),
+    ("Z", 1), ("Z", 3), ("D", 7), ("keep", 0, 4), ("relay", 7), ("forward", "F", 1),
+    ("finish", 0, 3), ("relay_across", 7), ("give", 0, 5), ("far", 0), ("far", 1), ("far", 2),
+    ("far", 3), ("keep", 0, 5), ("finish", 0, 4), ("far", 4), ("give", 0, 6), ("finish", 0, 5),
+    ("far", 5), ("keep", 0, 6), ("P", 1), ("P", 3), ("finish", 0, 6), ("far", 6),
+    ("forward", "P", 1), ("give", 1, 6), ("forward", "P", 3), ("keep", 1, 0), ("give", 0, 7),
+    ("keep", 0, 7), ("keep", 1, 5), ("keep", 1, 7), ("keep", 1, 3), ("keep", 1, 4),
+    ("give", 1, 1), ("keep", 1, 2), ("keep", 1, 6), ("finish", 0, 7), ("far", 7),
+    ("finish", 1, 6), ("keep", 1, 1), ("give", 1, 3), ("finish", 1, 1), ("last", 1),
+    ("give", 1, 7), ("finish", 1, 3), ("give", 1, 4), ("finish", 1, 7), ("give", 1, 0),
+    ("last", 3), ("finish", 1, 4), ("give", 1, 5), ("last", 4), ("finish", 1, 0), ("last", 0),
+    ("give", 1, 2), ("finish", 1, 5), ("last", 5), ("last", 6), ("finish", 1, 2), ("last", 2),
+    ("last", 7),
 )
 
 
@@ -57,7 +58,7 @@
     return tokens_product(all_tokens, lax.all_gather(columns, "row", axis=0, tiled=True))
 
 
-def encode(src, dst):
+def encode(src, dst, undo_row):
     rows, width = src.shape
 
     def strip(s):
@@ -67,10 +68,9 @@
         0, rows // STRIP, lambda s, m: jnp.maximum(m, jnp.abs(src[strip(s), :])),
         jnp.zeros((STRIP, width), jnp.float32),
     )
-    top = jnp.max(top, axis=0, keepdims=True)
-    undo = (jnp.maximum(top, 1e-30) * (1.0 / PEAK)).astype(jnp.bfloat16)
-    dst[pl.ds(rows, PAD), :] = jnp.broadcast_to(undo, (PAD, width))
-    scale = 1.0 / undo.astype(jnp.float32)
+    undo = jnp.maximum(jnp.max(top, axis=0, keepdims=True), 1e-30) * (1.0 / PEAK)
+    undo_row[...] = undo
+    scale = 1.0 / undo
 
     @pl.loop(0, rows // STRIP)
     def _(s):
@@ -82,11 +82,10 @@
         dst[strip(s), :] = jnp.where(t < 0, -u, u).astype(jnp.bfloat16)
 
 
-def decode_add(src, into):
-    rows = into.shape[0]
-    undo = src[pl.ds(rows, PAD), :].astype(jnp.float32)[:1]
-
-    @pl.loop(0, rows // STRIP)
+def decode_add(src, undo_row, into):
+    undo = undo_row[...]
+
+    @pl.loop(0, into.shape[0] // STRIP)
     def _(s):
         span = pl.ds(pl.multiple_of(s * STRIP, STRIP), STRIP)
         b = src[span, :].astype(jnp.float32)
@@ -97,9 +96,9 @@
 
 def kernel(
     lines, cols, feat, cot, out,
-    fall, dall, tmp, ysend, yrecv, acc, msend, mrecv,
+    fall, dall, tmp, ysend, yrecv, yu_out, yu_in, acc, msend, mrecv, mu_out, mu_in,
     fl, fz_s, fz_r, fx_s, fx_r, fm_s, fm_r,
-    dl, dx_s, dx_r, dz_s, dz_r, y_s, y_r, m_s, m_r, o_s,
+    dl, dx_s, dx_r, dz_s, dz_r, y_s, y_r, yu_s, yu_r, m_s, m_r, mu_s, mu_r,
 ):
     row = lax.axis_index("row")
     col = lax.axis_index("col")
@@ -110,8 +109,13 @@
     inner = (z > 0) & (z < lines - 1)
     tok = feat.shape[0]
     half = fall.shape[2]
-    chunks, _, chunk = dall.shape
-    width = chunks * chunk
+    chunks = len(WIDTHS)
+    width = dall.shape[1]
+    part = width // PARTS
+
+    def cols_of(j):
+        return pl.ds(sum(WIDTHS[:j]) * part, WIDTHS[j] * part)
+
 
     def at_row(zz, yy):
         return {"row": zz * 2 + yy, "col": col}
@@ -164,31 +168,48 @@
         return remote(src, block, fm_s.at[q, other, k], fm_r.at[q, other, k], at_col(MATE))
 
     def d_cols(cc, j):
-        return cot.at[:, pl.ds(pl.multiple_of(cc * width + j * chunk, chunk), chunk)]
+        first = pl.multiple_of(cc * width + sum(WIDTHS[:j]) * part, part)
+        return cot.at[:, pl.ds(first, WIDTHS[j] * part)]
 
     def d_own(j):
-        return pltpu.make_async_copy(d_cols(col, j), dall.at[j, slot(here, col)], dl.at[j])
+        return pltpu.make_async_copy(d_cols(col, j), dall.at[slot(here, col), cols_of(j)], dl.at[j])
 
     def d_send(j, k):
         return remote(
-            d_cols(col_of[k], j), dall.at[j, slot(here, col)],
+            d_cols(col_of[k], j), dall.at[slot(here, col), cols_of(j)],
             dx_s.at[j, k], dx_r.at[j, k], at_col(k),
         )
 
     def d_pair(j, k):
-        block = dall.at[j, slot(here, col_of[k])]
+        block = dall.at[slot(here, col_of[k]), cols_of(j)]
         return remote(
             block if k else d_cols(col, j), block, dz_s.at[j, k], dz_r.at[j, k], pair
         )
 
-    def y_copy(g, j):
-        return remote(ysend.at[g, j], yrecv.at[g, j], y_s.at[g, j], y_r.at[g, j], partner)
-
-    def m_copy(j):
-        return remote(msend.at[j], mrecv.at[j], m_s.at[j], m_r.at[j], mirror)
-
-    def out_copy(j):
-        return pltpu.make_async_copy(acc.at[1, j], out.at[:, pl.ds(j * chunk, chunk)], o_s.at[j])
+    def y_copies(g, j):
+        c = cols_of(j)
+        return (
+            remote(yu_out.at[g, :, c], yu_in.at[g, :, c], yu_s.at[g, j], yu_r.at[g, j], partner),
+            remote(ysend.at[g, :, c], yrecv.at[g, :, c], y_s.at[g, j], y_r.at[g, j], partner),
+        )
+
+    def m_copies(j):
+        c = cols_of(j)
+        return (
+            remote(mu_out.at[:, c], mu_in.at[:, c], mu_s.at[j], mu_r.at[j], mirror),
+            remote(msend.at[:, c], mrecv.at[:, c], m_s.at[j], m_r.at[j], mirror),
+        )
+
+    def start(copies):
+        for copy in copies:
+            copy.start()
+
+    def receive(copies):
+        for copy in copies:
+            copy.wait_recv()
+
+    def total(g, j):
+        return (out if g else acc).at[:, cols_of(j)]
 
     ready = set()
 
@@ -243,33 +264,36 @@
 
     def do_give(g, j):
         arrive(g, j)
-        tmp[...] = tokens_product(fall[g], dall[j])
-        encode(tmp, ysend.at[g, j])
-        y_copy(g, j).start()
+        c = cols_of(j)
+        made = tmp.at[:, pl.ds(0, c.size)]
+        made[...] = tokens_product(fall[g], dall[:, c])
+        encode(made, ysend.at[g, :, c], yu_out.at[g, :, c])
+        start(y_copies(g, j))
 
     def do_keep(g, j):
         arrive(2 + g, j)
-        acc[g, j] = tokens_product(fall[2 + g], dall[j])
+        total(g, j)[...] = tokens_product(fall[2 + g], dall[:, cols_of(j)])
 
     def do_finish(g, j):
-        y_copy(g, j).wait_recv()
-        decode_add(yrecv.at[g, j], acc.at[g, j])
+        receive(y_copies(g, j))
+        c = cols_of(j)
+        decode_add(yrecv.at[g, :, c], yu_in.at[g, :, c], total(g, j))
         if g == 0:
-            encode(acc.at[0, j], msend.at[j])
+            encode(total(0, j), msend.at[:, c], mu_out.at[:, c])
 
             @pl.when(inner)
             def _():
-                m_copy(j).start()
+                start(m_copies(j))
 
     def do_far(j):
         @pl.when(~inner)
         def _():
-            m_copy(j).start()
+            start(m_copies(j))
 
     def do_last(j):
-        m_copy(j).wait_recv()
-        decode_add(mrecv.at[j], acc.at[1, j])
-        out_copy(j).start()
+        receive(m_copies(j))
+        c = cols_of(j)
+        decode_add(mrecv.at[:, c], mu_in.at[:, c], total(1, j))
 
     run = {
         "Z": do_Z, "F": do_F, "P": do_P, "far": do_far, "D": do_D, "forward": do_forward, "relay": do_relay,
@@ -291,10 +315,8 @@
             d_pair(j, k).wait_send()
         for k in range(1, cols):
             d_send(j, k).wait_send()
-        for g in range(2):
-            y_copy(g, j).wait_send()
-        m_copy(j).wait_send()
-        out_copy(j).wait()
+        for copy in y_copies(0, j) + y_copies(1, j) + m_copies(j):
+            copy.wait_send()
 
 
 def sizes(row_count, cols, features, cotangent):
@@ -307,29 +329,30 @@
 
 def fused(row_count, cols, features, cotangent):
     lines, tokens, rows, width = sizes(row_count, cols, features, cotangent)
-    chunks, chunk = CHUNKS, width // CHUNKS
-    half = rows // 2
+    chunks, half = len(WIDTHS), rows // 2
     dma = pltpu.SemaphoreType.DMA
-    coded = pltpu.VMEM((2, chunks, half + PAD, chunk), jnp.bfloat16)
-    moved = pltpu.VMEM((chunks, half + PAD, chunk), jnp.bfloat16)
+    coded = pltpu.VMEM((2, half, width), jnp.bfloat16)
+    moved = pltpu.VMEM((half, width), jnp.bfloat16)
+    coded_undo = pltpu.VMEM((2, 1, width), jnp.float32)
+    moved_undo = pltpu.VMEM((1, width), jnp.float32)
     return pl.pallas_call(
         functools.partial(kernel, lines, cols),
-        out_shape=jax.ShapeDtypeStruct((half, width), jnp.float32),
+        out_shape=pltpu.VMEM((half, width), jnp.float32),
         in_specs=[pl.BlockSpec(memory_space=pl.ANY)] * 2,
-        out_specs=pl.BlockSpec(memory_space=pl.ANY),
+        out_specs=pl.BlockSpec(memory_space=pltpu.VMEM),
         scratch_shapes=[
             pltpu.VMEM((4, tokens, half), jnp.bfloat16),
-            pltpu.VMEM((chunks, tokens, chunk), jnp.bfloat16),
-            pltpu.VMEM((half, chunk), jnp.float32),
-            coded, coded,
-            pltpu.VMEM((2, chunks, half, chunk), jnp.float32),
-            moved, moved,
+            pltpu.VMEM((tokens, width), jnp.bfloat16),
+            pltpu.VMEM((half, max(WIDTHS) * width // PARTS), jnp.float32),
+            coded, coded, coded_undo, coded_undo,
+            pltpu.VMEM((half, width), jnp.float32),
+            moved, moved, moved_undo, moved_undo,
             dma((4,)), dma((4,)), dma((4,)),
             dma((4, 2)), dma((4, 2)), dma((4, 2, 2)), dma((4, 2, 2)),
             dma((chunks,)), dma((chunks, cols)), dma((chunks, cols)),
             dma((chunks, cols)), dma((chunks, cols)),
-            dma((2, chunks)), dma((2, chunks)), dma((chunks,)), dma((chunks,)),
-            dma((chunks,)),
+            dma((2, chunks)), dma((2, chunks)), dma((2, chunks)), dma((2, chunks)),
+            dma((chunks,)), dma((chunks,)), dma((chunks,)), dma((chunks,)),
         ],
         compiler_params=pltpu.CompilerParams(
             collective_id=0, has_side_effects=True, vmem_limit_bytes=VMEM_MOST
@@ -338,12 +361,12 @@
 
 
 def fits(row_count, cols, features, cotangent):
-    if row_count != 8 or cols != 4 or cotangent.shape[1] % (cols * CHUNKS * 128):
+    if row_count != 8 or cols != 4 or cotangent.shape[1] % (cols * PARTS * 128):
         return False
     if features.shape[1] % (row_count * 128) or features.shape[0] % 16:
         return False
     lines, tokens, rows, width = sizes(row_count, cols, features, cotangent)
-    held = 2 * tokens * (2 * rows + width) + 11 * rows * width + 4 * rows * width // CHUNKS
+    held = 2 * tokens * (2 * rows + width) + 11 * rows * width + 4 * rows * width // 8
     return held <= VMEM_MOST
 
 

time: 150 us -> 146 us (0.973)
  local copies, waits for them, and re-layouts: 4.7 us -> 2.02 us
  Pallas kernels: 146 us -> 144 us
    unnamed x1, local copies, waits for them, and re-layouts: 4.7 us -> 2.02 us
    pallas_call x1, Pallas kernels: 146 us -> 144 us  [fused(): pl.pallas_call(functools.partial(kernel, lines, cols), out_shape=pltpu.VM...]
where the time goes in v4:
time: 146 us
  Pallas kernels  144 us (99%)
  local copies, waits for them, and re-layouts  2.02 us (1%)
    pallas_call x1, Pallas kernels, fused(): pl.pallas_call(functools.partial(kernel, lines, cols), out_shape=pltpu.VM...  144 us

profile of v4, /device:TPU:9, one launch (start us, length us, event | category | flops | bytes accessed | tf_op | source)
XLA Modules:
  0.0 145.9 jit_solution(7928088962814394587)
XLA Ops:
  0.0 143.8 %shard_map.28 = f32[512,2048]{1,0:T(8,128)S(1)} custom-call(bf16[192,4096]{1,0:T(8,128)(2,1)} %feat.1, bf16[192,8192]{1,0:T(8,128)(2,1)} %cot.1), custom_call_target="tpu_custom_call" | custom-call | tf_op jit(solution)/shard_map/pallas_call | solution.py:338
  143.8 2.0 %copy.4 = f32[512,2048]{1,0:T(8,128)} copy(f32[512,2048]{1,0:T(8,128)S(1)} %shard_map.28) | data formatting | bytes 8388608

commit v5 on v4

--- a/solution.py
+++ b/solution.py
@@ -97,8 +97,7 @@
 def kernel(
     lines, cols, feat, cot, out,
     fall, dall, tmp, ysend, yrecv, yu_out, yu_in, acc, msend, mrecv, mu_out, mu_in,
-    fl, fz_s, fz_r, fx_s, fx_r, fm_s, fm_r,
-    dl, dx_s, dx_r, dz_s, dz_r, y_s, y_r, yu_s, yu_r, m_s, m_r, mu_s, mu_r,
+    f_s, fz_r, fx_r, fm_r, d_s, dx_r, dz_r, y_s, y_r, yu_s, yu_r, m_s, m_r, mu_s, mu_r,
 ):
     row = lax.axis_index("row")
     col = lax.axis_index("col")
@@ -149,10 +148,10 @@
         return feat.at[:, pl.ds(pl.multiple_of((wanted * 2 + yy) * half, half), half)]
 
     def f_own(q):
-        return pltpu.make_async_copy(f_cols(z, q), fall.at[q, slot(here, col)], fl.at[q])
+        return pltpu.make_async_copy(f_cols(z, q), fall.at[q, slot(here, col)], fm_r.at[q])
 
     def f_pair(q):
-        return remote(f_cols(near, q), fall.at[q, slot(here, col)], fz_s.at[q], fz_r.at[q], pair)
+        return remote(f_cols(near, q), fall.at[q, slot(here, col)], f_s.at[0], fz_r.at[q], pair)
 
     def f_block(q, other, k):
         return fall.at[q, slot(1 - here if other else here, col_of[k])]
@@ -160,44 +159,55 @@
     def f_across(q, other):
         block = f_block(q, other, 0)
         src = block if other else f_cols(z, q)
-        return remote(src, block, fx_s.at[q, other], fx_r.at[q, other], at_col(ACROSS))
+        return remote(src, block, f_s.at[0], fx_r.at[q, other], at_col(ACROSS))
 
     def f_mate(q, other, k):
         block = f_block(q, other, ACROSS * k)
         src = f_cols(z, q) if not other and not k else block
-        return remote(src, block, fm_s.at[q, other, k], fm_r.at[q, other, k], at_col(MATE))
+        return remote(src, block, f_s.at[0], fm_r.at[q], at_col(MATE))
 
     def d_cols(cc, j):
         first = pl.multiple_of(cc * width + sum(WIDTHS[:j]) * part, part)
         return cot.at[:, pl.ds(first, WIDTHS[j] * part)]
 
     def d_own(j):
-        return pltpu.make_async_copy(d_cols(col, j), dall.at[slot(here, col), cols_of(j)], dl.at[j])
+        return pltpu.make_async_copy(d_cols(col, j), dall.at[slot(here, col), cols_of(j)], dz_r.at[j])
 
     def d_send(j, k):
         return remote(
             d_cols(col_of[k], j), dall.at[slot(here, col), cols_of(j)],
-            dx_s.at[j, k], dx_r.at[j, k], at_col(k),
+            d_s.at[0], dx_r.at[j, k // ACROSS], at_col(k),
         )
 
+    def d_block(j, k):
+        if k < ACROSS:
+            return dall.at[slot(here, col_of[k]), cols_of(j)]
+        first = (here * cols + (col // 2 * 2 + 2) % cols) * tok
+        return dall.at[pl.ds(pl.multiple_of(first, tok), 2 * tok), cols_of(j)]
+
+    def d_recv(j, k):
+        block = d_block(j, k)
+        return remote(block, block, d_s.at[0], dx_r.at[j, k // ACROSS], at_col(k))
+
     def d_pair(j, k):
-        block = dall.at[slot(here, col_of[k]), cols_of(j)]
-        return remote(
-            block if k else d_cols(col, j), block, dz_s.at[j, k], dz_r.at[j, k], pair
+        block = d_block(j, k)
+        return remote(block if k else d_cols(col, j), block, d_s.at[0], dz_r.at[j], pair)
+
+    def bytes_of(block, sem):
+        return pltpu.make_async_copy(block, block, sem)
+
+    def y_copies(g, j):
+        c = cols_of(j)
+        return (
+            remote(yu_out.at[g, :, c], yu_in.at[g, :, c], yu_s.at[0], yu_r.at[g, j], partner),
+            remote(ysend.at[g, :, c], yrecv.at[g, :, c], y_s.at[0], y_r.at[g, j], partner),
         )
 
-    def y_copies(g, j):
+    def m_copies(j):
         c = cols_of(j)
         return (
-            remote(yu_out.at[g, :, c], yu_in.at[g, :, c], yu_s.at[g, j], yu_r.at[g, j], partner),
-            remote(ysend.at[g, :, c], yrecv.at[g, :, c], y_s.at[g, j], y_r.at[g, j], partner),
-        )
-
-    def m_copies(j):
-        c = cols_of(j)
-        return (
-            remote(mu_out.at[:, c], mu_in.at[:, c], mu_s.at[j], mu_r.at[j], mirror),
-            remote(msend.at[:, c], mrecv.at[:, c], m_s.at[j], m_r.at[j], mirror),
+            remote(mu_out.at[:, c], mu_in.at[:, c], mu_s.at[0], mu_r.at[j], mirror),
+            remote(msend.at[:, c], mrecv.at[:, c], m_s.at[0], m_r.at[j], mirror),
         )
 
     def start(copies):
@@ -220,14 +230,9 @@
 
     def arrive(q, j):
         if once(("F", q)):
-            f_own(q).wait()
-            for other in range(2):
-                for k in range(2):
-                    f_mate(q, other, k).wait_recv()
+            bytes_of(fall.at[q, pl.ds(0, 5 * tok)], fm_r.at[q]).wait()
         if once(("D", j)):
-            d_own(j).wait()
-            for k in range(cols):
-                d_pair(j, k).wait_recv()
+            bytes_of(dall.at[pl.ds(0, 5 * tok), cols_of(j)], dz_r.at[j]).wait()
 
     def do_Z(q):
         f_pair(q).start()
@@ -254,13 +259,12 @@
         f_mate(q, other, 1).start()
 
     def do_relay(j):
-        d_send(j, MATE).wait_recv()
+        d_recv(j, MATE).wait_recv()
         d_pair(j, MATE).start()
 
     def do_relay_across(j):
-        for k in (2, 3):
-            d_send(j, k).wait_recv()
-            d_pair(j, k).start()
+        d_recv(j, ACROSS).wait_recv()
+        d_pair(j, ACROSS).start()
 
     def do_give(g, j):
         arrive(g, j)
@@ -304,19 +308,10 @@
         with jax.named_scope(name + "".join(str(w) for w in which)):
             run[name](*which)
 
-    for q in range(4):
-        f_pair(q).wait_send()
-        for other in range(2):
-            f_across(q, other).wait_send()
-            for k in range(2):
-                f_mate(q, other, k).wait_send()
-    for j in range(chunks):
-        for k in range(cols):
-            d_pair(j, k).wait_send()
-        for k in range(1, cols):
-            d_send(j, k).wait_send()
-        for copy in y_copies(0, j) + y_copies(1, j) + m_copies(j):
-            copy.wait_send()
+    bytes_of(fall.at[:, pl.ds(0, 7 * tok)], f_s.at[0]).wait()
+    bytes_of(dall.at[pl.ds(0, 7 * tok)], d_s.at[0]).wait()
+    for sent, sem in ((ysend, y_s), (yu_out, yu_s), (msend, m_s), (mu_out, mu_s)):
+        bytes_of(sent, sem.at[0]).wait()
 
 
 def sizes(row_count, cols, features, cotangent):
@@ -347,12 +342,10 @@
             coded, coded, coded_undo, coded_undo,
             pltpu.VMEM((half, width), jnp.float32),
             moved, moved, moved_undo, moved_undo,
-            dma((4,)), dma((4,)), dma((4,)),
-            dma((4, 2)), dma((4, 2)), dma((4, 2, 2)), dma((4, 2, 2)),
-            dma((chunks,)), dma((chunks, cols)), dma((chunks, cols)),
-            dma((chunks, cols)), dma((chunks, cols)),
-            dma((2, chunks)), dma((2, chunks)), dma((2, chunks)), dma((2, chunks)),
-            dma((chunks,)), dma((chunks,)), dma((chunks,)), dma((chunks,)),
+            dma((1,)), dma((4,)), dma((4, 2)), dma((4,)),
+            dma((1,)), dma((chunks, 2)), dma((chunks,)),
+            dma((1,)), dma((2, chunks)), dma((1,)), dma((2, chunks)),
+            dma((1,)), dma((chunks,)), dma((1,)), dma((chunks,)),
         ],
         compiler_params=pltpu.CompilerParams(
             collective_id=0, has_side_effects=True, vmem_limit_bytes=VMEM_MOST

time: 146 us -> 144 us (0.986)
  Pallas kernels: 144 us -> 142 us
    pallas_call x1, Pallas kernels: 144 us -> 142 us  [fused(): pl.pallas_call(functools.partial(kernel, lines, cols), out_shape=pltpu.VM...]
where the time goes in v5:
time: 144 us
  Pallas kernels  142 us (99%)
  local copies, waits for them, and re-layouts  2.02 us (1%)
    pallas_call x1, Pallas kernels, fused(): pl.pallas_call(functools.partial(kernel, lines, cols), out_shape=pltpu.VM...  142 us

profile of v5, /device:TPU:9, one launch (start us, length us, event | category | flops | bytes accessed | tf_op | source)
XLA Modules:
  0.0 143.9 jit_solution(14381475735218665724)
XLA Ops:
  0.0 141.9 %shard_map.28 = f32[512,2048]{1,0:T(8,128)S(1)} custom-call(bf16[192,4096]{1,0:T(8,128)(2,1)} %feat.1, bf16[192,8192]{1,0:T(8,128)(2,1)} %cot.1), custom_call_target="tpu_custom_call" | custom-call | tf_op jit(solution)/shard_map/pallas_call | solution.py:333
  141.9 2.0 %copy.4 = f32[512,2048]{1,0:T(8,128)} copy(f32[512,2048]{1,0:T(8,128)S(1)} %shard_map.28) | data formatting | bytes 8388608

commit v6 on v5

--- a/solution.py
+++ b/solution.py
@@ -10,8 +10,8 @@
 MESH = pl.DeviceIdType.MESH
 WIDTHS = (1, 1, 1, 1, 1, 1, 1, 1)
 PARTS = sum(WIDTHS)
-STRIP = 32
-PEAK = 181.0
+STRIP = 64
+PEAK = 250.0
 VMEM_MOST = 58 * 1024 * 1024
 
 
@@ -68,7 +68,7 @@
         0, rows // STRIP, lambda s, m: jnp.maximum(m, jnp.abs(src[strip(s), :])),
         jnp.zeros((STRIP, width), jnp.float32),
     )
-    undo = jnp.maximum(jnp.max(top, axis=0, keepdims=True), 1e-30) * (1.0 / PEAK)
+    undo = jnp.maximum(jnp.max(top, axis=0, keepdims=True), 4e-36) * (1.0 / PEAK)
     undo_row[...] = undo
     scale = 1.0 / undo
 

time: 144 us -> 144 us (level)
  no operation moved by 1% of the time
where the time goes in v6:
time: 144 us
  Pallas kernels  142 us (99%)
  local copies, waits for them, and re-layouts  2.02 us (1%)
    pallas_call x1, Pallas kernels, fused(): pl.pallas_call(functools.partial(kernel, lines, cols), out_shape=pltpu.VM...  142 us

profile of v6, /device:TPU:9, one launch (start us, length us, event | category | flops | bytes accessed | tf_op | source)
XLA Modules:
  0.0 143.8 jit_solution(9510672892249991979)
XLA Ops:
  0.0 141.8 %shard_map.28 = f32[512,2048]{1,0:T(8,128)S(1)} custom-call(bf16[192,4096]{1,0:T(8,128)(2,1)} %feat.1, bf16[192,8192]{1,0:T(8,128)(2,1)} %cot.1), custom_call_target="tpu_custom_call" | custom-call | tf_op jit(solution)/shard_map/pallas_call | solution.py:333
  141.8 2.0 %copy.4 = f32[512,2048]{1,0:T(8,128)} copy(f32[512,2048]{1,0:T(8,128)S(1)} %shard_map.28) | data formatting | bytes 8388608
